TPU v7x, 32 devices: a whole 2x2x4 slice. The times are simulated.
32 devices in a mesh: ctx: 4 (over x, core), vocab: 8 (over z, y).
Axes of the slice: x: 2, y: 2, z: 4, core: 2. Of those that a mesh axis runs over, the one named last changes fastest.
Arguments:
- hidden: bfloat16 [256, 2, 7168], P('ctx', None, 'vocab'), may hold values from -30 to 30
- head: bfloat16 [7168, 16384], P('ctx', 'vocab'), may hold values from -0.15 to 0.15
- targets: int32 [256, 2], P('ctx'), may hold values from 0 to 16383
- loss_weight: float32 [256, 2], P('ctx'), may hold values from 16 to 256
Outputs:
- token_loss: float32 [256, 2], P('ctx')
- grad_hidden: bfloat16 [256, 2, 7168], P('ctx', None, 'vocab')
All inputs are finite; a program needn't handle non-finite values.
Results may differ from a plain program's by a relative error of at most 0.0046.
Values may be sent and summed in bfloat16 or wider, within the bound.
No kernel may reach another device: no remote copies, remote signals or barrier semaphores. Data moves between devices by JAX's collectives and lax.ppermute only.
A program may use at most 64 MiB of HBM per device.

v0:
```python
import jax
import jax.numpy as jnp
from jax import lax
from jax.sharding import PartitionSpec as P


def body(hidden, head, targets, loss_weight):
    group_rows = hidden.shape[0]
    depth_count = hidden.shape[1]
    flat_count = group_rows * depth_count
    vocab_index = lax.axis_index("vocab")
    vocab_local = head.shape[1]
    flat_hidden = hidden.reshape(flat_count, hidden.shape[2])
    flat_targets = targets.reshape(flat_count)
    flat_weights = loss_weight.reshape(flat_count)
    whole_width = lax.all_gather(flat_hidden, "vocab", axis=1, tiled=True)
    width_slab = lax.all_to_all(whole_width, "ctx", split_axis=1, concat_axis=0, tiled=True)
    logits = lax.psum_scatter(
        jnp.dot(width_slab, head, preferred_element_type=jnp.float32),
        "ctx",
        scatter_dimension=0,
        tiled=True,
    )
    columns = vocab_index * vocab_local + lax.broadcasted_iota(jnp.int32, logits.shape, 1)
    target_hit = columns == flat_targets[:, None]
    local_max = jnp.max(logits, axis=1)
    local_target = jnp.sum(jnp.where(target_hit, logits, 0.0), axis=1)
    row_max = lax.pmax(local_max, "vocab")
    local_sum = jnp.sum(jnp.exp(logits - row_max[:, None]), axis=1)
    sum_exp, target_logit = lax.psum((local_sum, local_target), "vocab")
    flat_loss = jnp.log(sum_exp) + row_max - target_logit
    token_loss = flat_loss.reshape(group_rows, depth_count)
    probabilities = jnp.exp(logits - row_max[:, None]) / sum_exp[:, None]
    dlogits = (flat_weights[:, None] * (probabilities - target_hit.astype(jnp.float32))).astype(
        jnp.bfloat16
    )
    grad_slab = lax.dot_general(
        lax.all_gather(dlogits, "ctx", axis=0, tiled=True),
        head,
        (((1,), (1,)), ((), ())),
        preferred_element_type=jnp.float32,
    )
    returned = lax.all_to_all(grad_slab, "ctx", split_axis=0, concat_axis=1, tiled=True)
    grad_width = lax.psum_scatter(returned, "vocab", scatter_dimension=1, tiled=True)
    grad_out = grad_width.astype(jnp.bfloat16).reshape(group_rows, depth_count, grad_width.shape[1])
    return (token_loss, grad_out)


def solution(mesh):
    return jax.shard_map(
        body,
        mesh=mesh,
        in_specs=(P("ctx", None, "vocab"), P("ctx", "vocab"), P("ctx", None), P("ctx", None)),
        out_specs=(P("ctx", None), P("ctx", None, "vocab")),
        check_vma=False,
    )
```

profile of v0, /device:TPU:0, one launch (start us, length us, event | category | flops | bytes accessed | tf_op | source)
XLA Modules:
  0.0 360.6 jit_solution(2139079968962147869)
XLA Ops:
  7.2 0.0 all-gather.3.cloned.1.call-start
  7.2 1.7 reshape.23
  8.9 0.0 reduce-scatter.3.cloned.1.call-start
  9.0 51.1 %all-gather.3.cloned.1.call-done = bf16[128,7168]{1,0:T(8,128)(2,1)} async-done(((bf16[128,896]{1,0:T(8,128)(2,1)}), bf16[128,7168]{1,0:T(8,128)(2,1)}) %all-gather.3.cloned.1.call-update) | async-done | bytes 1835024 | tf_op jit(solution)/shard_map/all_gather | solution.py:16
  60.1 3.3 copy.21
  63.4 26.1 %all_to_all.38 = bf16[128,4,1792]{0,2,1:T(8,128)(2,1)} all-to-all(bf16[128,4,1792]{0,2,1:T(8,128)(2,1)S(1)} %bitcast.12), channel_id=1, replica_groups=mesh['ctx'=4,'vocab'=8] {'ctx'}, dimensions={1} | all-to-all | bytes 3670016 | tf_op jit(solution)/shard_map/all_to_all | solution.py:17
  89.4 2.8 copy.22
  92.2 8.6 %fusion.5 = f32[512,2048]{1,0:T(8,128)} fusion(bf16[512,1792]{1,0:T(8,128)(2,1)S(1)} %bitcast.15, bf16[1792,2048]{1,0:T(8,128)(2,1)} %param.5), kind=kOutput, calls=%fused_computation.10 | convolution fusion | flops 3758096384 | bytes 13369344 | tf_op jit(solution)/shard_map/dot_general | solution.py:19
  100.8 0.0 all-gather.5.cloned.1.call-start
  100.9 0.6 copy-done
  101.5 0.1 copy.23
  101.5 0.1 eq.10
  101.7 0.1 copy.24
  101.8 0.1 mul.14
  101.9 41.5 %reduce-scatter.3.cloned.1.call-done = f32[128,2048]{1,0:T(8,128)} async-done(((f32[512,2048]{1,0:T(8,128)}), f32[128,2048]{1,0:T(8,128)}) %reduce-scatter.3.cloned.1.call-update) | async-done | bytes 1048592 | tf_op jit(solution)/shard_map/reduce_scatter | solution.py:18
  143.5 1.4 reduce_max.9
  144.8 21.4 %pmax.7 = f32[128]{0:T(128)S(1)} all-reduce(f32[128]{0:T(128)S(1)} %reduce_max.9), channel_id=1, replica_groups=mesh['ctx'=4,'vocab'=8] {'vocab'}, use_global_device_ids=true, to_apply=%region_2.3 | all-reduce | flops 128 | bytes 1024 | tf_op jit(solution)/shard_map/pmax | solution.py:28
  166.2 1.6 fusion.4
  167.8 17.1 %all-reduce = (f32[128]{0:T(128)S(1)}, f32[128]{0:T(128)S(1)}) all-reduce(f32[128]{0:T(128)S(1)} %get-tuple-element.11, f32[128]{0:T(128)S(1)} %get-tuple-element.10), channel_id=1, replica_groups=mesh['ctx'=4,'vocab'=8] {'vocab'}, use_global_device_ids=true, to_apply=%region_6.7 | all-reduce | flops 256 | bytes 2048 | tf_op jit(solution)/shard_map/psum | solution.py:30
  184.9 2.4 fusion.3
  187.4 0.0 reduce-scatter.5.cloned.1.call-start
  187.4 20.4 %all-gather.5.cloned.1.call-done = bf16[512,2048]{1,0:T(8,128)(2,1)} async-done(((bf16[128,2048]{1,0:T(8,128)(2,1)}), bf16[512,2048]{1,0:T(8,128)(2,1)}) %all-gather.5.cloned.1.call-update) | async-done | bytes 2097168 | tf_op jit(solution)/shard_map/all_gather | solution.py:38
  207.8 9.5 %fusion.6 = f32[512,1792]{1,0:T(8,128)} fusion(bf16[512,2048]{1,0:T(8,128)(2,1)} %all-gather.5.cloned.1.call-done, bf16[1792,2048]{1,0:T(8,128)(2,1)} %param.5), kind=kOutput, calls=%fused_computation.11 | convolution fusion | flops 3758096384 | bytes 13107200 | tf_op jit(solution)/shard_map/dot_general | solution.py:37
  217.4 5.1 %copy.25 = f32[4,128,1792]{1,2,0:T(8,128)} copy(f32[4,128,1792]{2,1,0:T(8,128)} %bitcast.14) | data formatting | bytes 7340032 | tf_op jit(solution)/shard_map/all_to_all | solution.py:43
  222.5 48.1 %all_to_all.39 = f32[4,128,1792]{1,2,0:T(8,128)} all-to-all(f32[4,128,1792]{1,2,0:T(8,128)} %copy.25), channel_id=1, replica_groups=mesh['ctx'=4,'vocab'=8] {'ctx'}, dimensions={0} | all-to-all | bytes 7340032 | tf_op jit(solution)/shard_map/all_to_all | solution.py:43
  270.6 0.0 reduce-scatter.5.cloned.1.call-update
  270.6 0.1 reshape.24
  270.8 0.6 copy.27
  271.4 80.7 %reduce-scatter.5.cloned.1.call-done = f32[128,896]{0,1:T(8,128)} async-done(((f32[128,7168]{0,1:T(8,128)}), f32[128,896]{0,1:T(8,128)}) %reduce-scatter.5.cloned.1.call-update) | async-done | bytes 458768 | tf_op jit(solution)/shard_map/reduce_scatter | solution.py:44
  352.1 1.0 convert_element_type.11
  353.1 0.2 copy.26
  353.3 0.8 reshape.25
  (8 shorter events, 0.1 us)
Async XLA Ops:
  7.2 52.9 %all-gather.3.cloned.1.call-start = ((), (), s32[]{:S(2)}) async-start(), calls=%async_computation.4 | async-start | bytes 2064384 | tf_op jit(solution)/shard_map/all_gather | solution.py:16
  8.9 134.5 %reduce-scatter.3.cloned.1.call-start = ((), (), s32[]{:S(2)}) async-start(), calls=%async_computation.5 | async-start | bytes 5242880 | tf_op jit(solution)/shard_map/reduce_scatter | solution.py:18
  100.8 0.7 copy-start
  100.8 0.9 copy-start.1
  100.8 107.0 %all-gather.5.cloned.1.call-start = ((), (), s32[]{:S(2)}) async-start(), calls=%async_computation.6 | async-start | bytes 2621440 | tf_op jit(solution)/shard_map/all_gather | solution.py:38
  187.4 164.7 %reduce-scatter.5.cloned.1.call-start = ((), (), s32[]{:S(2)}) async-start(), calls=%async_computation.7 | async-start | bytes 4128768 | tf_op jit(solution)/shard_map/reduce_scatter | solution.py:44
Sparse Core Ops, SparseCore 0:
  10.8 49.2 all-gather.2
  100.9 42.4 reduce-scatter.2
  187.5 20.3 all-gather.4
  270.7 81.2 reduce-scatter.4
where the time goes:
time: 361 us
  waiting for transfers between devices  194 us (54%)
  blocking collectives  113 us (31%)
  matrix products  18.1 us (5%)
  local copies, waits for them, and re-layouts  15.7 us (4%)
  between operations  13.8 us (4%)
  other arithmetic  6.43 us (2%)
    reduce_scatter x1, waiting for transfers between devices, body(): lax.psum_scatter(returned, 'vocab', scatter_dimension=1, tiled=True)  80.7 us
    all_gather x1, waiting for transfers between devices, body(): whole_width = lax.all_gather(flat_hidden, 'vocab', axis=1, tiled=True)  51.1 us
    all_to_all x1, blocking collectives, body(): lax.all_to_all(grad_slab, 'ctx', split_axis=0, concat_axis=1, tiled=True)  48.1 us
    reduce_scatter x1, waiting for transfers between devices, body(): lax.psum_scatter(jnp.dot(width_slab, head, preferred_element_type=jnp.flo...  41.5 us
    all_to_all x1, blocking collectives, body(): lax.all_to_all(whole_width, 'ctx', split_axis=1, concat_axis=0, tiled=True)  26.1 us
    pmax x1, blocking collectives, body(): row_max = lax.pmax(local_max, 'vocab')  21.4 us
    all_gather x1, waiting for transfers between devices, body(): lax.all_gather(dlogits, 'ctx', axis=0, tiled=True)  20.4 us
    psum x1, blocking collectives, body(): sum_exp, target_logit = lax.psum((local_sum, local_target), 'vocab')  17.1 us
  transfers between devices with their start and end apart: 4, of which 4 were waited for; matrix products, arithmetic and copies ran while one was open for 0% of the time, Pallas kernels for 0%

commit v1 on v0

--- a/solution.py
+++ b/solution.py
@@ -2,6 +2,16 @@
 import jax.numpy as jnp
 from jax import lax
 from jax.sharding import PartitionSpec as P
+
+place_plate = lambda mat, out_dim, k_dim: jnp.concatenate(
+    lax.all_to_all(
+        jnp.stack(jnp.split(mat, lax.axis_size("ctx"), axis=out_dim), axis=0),
+        axis_name="ctx",
+        split_axis=0,
+        concat_axis=0,
+    ),
+    axis=k_dim,
+)
 
 
 def body(hidden, head, targets, loss_weight):
@@ -40,7 +50,7 @@
         (((1,), (1,)), ((), ())),
         preferred_element_type=jnp.float32,
     )
-    returned = lax.all_to_all(grad_slab, "ctx", split_axis=0, concat_axis=1, tiled=True)
+    returned = place_plate(grad_slab, 0, 1)
     grad_width = lax.psum_scatter(returned, "vocab", scatter_dimension=1, tiled=True)
     grad_out = grad_width.astype(jnp.bfloat16).reshape(group_rows, depth_count, grad_width.shape[1])
     return (token_loss, grad_out)

time: 361 us -> 358 us (level)
    reshape x0 -> x1, local copies, waits for them, and re-layouts: none -> 5.14 us  [jnp.concatenate(lax.all_to_all(jnp.stack(jnp.split(mat, lax.axis_size('ct...]
    all_to_all x1 -> x0, local copies, waits for them, and re-layouts: 5.12 us -> none  [body(): lax.all_to_all(grad_slab, 'ctx', split_axis=0, concat_axis=1, tiled=True)]
where the time goes in v1:
time: 358 us; the launch traced here: 357 us
  waiting for transfers between devices  194 us (54%)
  blocking collectives  110 us (31%)
  matrix products  16.3 us (5%)
  local copies, waits for them, and re-layouts  16 us (4%)
  between operations  13.9 us (4%)
  other arithmetic  6.79 us (2%)
    reduce_scatter x1, waiting for transfers between devices, body(): lax.psum_scatter(returned, 'vocab', scatter_dimension=1, tiled=True)  80.7 us
    all_gather x1, waiting for transfers between devices, body(): whole_width = lax.all_gather(flat_hidden, 'vocab', axis=1, tiled=True)  51.1 us
    all_to_all x1, blocking collectives, lax.all_to_all(jnp.stack(jnp.split(mat, lax.axis_size('ctx'), axis=out_di...  45.9 us
    reduce_scatter x1, waiting for transfers between devices, body(): lax.psum_scatter(jnp.dot(width_slab, head, preferred_element_type=jnp.flo...  41.5 us
    all_to_all x1, blocking collectives, body(): lax.all_to_all(whole_width, 'ctx', split_axis=1, concat_axis=0, tiled=True)  26.1 us
    pmax x1, blocking collectives, body(): row_max = lax.pmax(local_max, 'vocab')  21.4 us
    all_gather x1, waiting for transfers between devices, body(): lax.all_gather(dlogits, 'ctx', axis=0, tiled=True)  20.4 us
    psum x1, blocking collectives, body(): sum_exp, target_logit = lax.psum((local_sum, local_target), 'vocab')  17.1 us
  transfers between devices with their start and end apart: 4, of which 4 were waited for; matrix products, arithmetic and copies ran while one was open for 0% of the time, Pallas kernels for 0%

profile of v1, /device:TPU:0, one launch (start us, length us, event | category | flops | bytes accessed | tf_op | source)
XLA Modules:
  0.0 357.3 jit_solution(14834097262518159521)
XLA Ops:
  7.2 1.7 reshape.26
  8.9 0.0 reduce-scatter.3.cloned.1.call-start
  9.0 51.1 %all-gather.3.cloned.1.call-done = bf16[128,7168]{1,0:T(8,128)(2,1)} async-done(((bf16[128,896]{1,0:T(8,128)(2,1)}), bf16[128,7168]{1,0:T(8,128)(2,1)}) %all-gather.3.cloned.1.call-update) | async-done | bytes 1835024 | tf_op jit(solution)/shard_map/all_gather | solution.py:26
  60.1 3.3 copy.21
  63.4 26.1 %all_to_all.24 = bf16[128,4,1792]{0,2,1:T(8,128)(2,1)} all-to-all(bf16[128,4,1792]{0,2,1:T(8,128)(2,1)S(1)} %bitcast.19), channel_id=1, replica_groups=mesh['ctx'=4,'vocab'=8] {'ctx'}, dimensions={1} | all-to-all | bytes 3670016 | tf_op jit(solution)/shard_map/all_to_all | solution.py:27
  89.4 2.8 copy.22
  92.2 8.6 %fusion.5 = f32[512,2048]{1,0:T(8,128)} fusion(bf16[512,1792]{1,0:T(8,128)(2,1)S(1)} %bitcast.21, bf16[1792,2048]{1,0:T(8,128)(2,1)} %param.5), kind=kOutput, calls=%fused_computation.15 | convolution fusion | flops 3758096384 | bytes 13369344 | tf_op jit(solution)/shard_map/dot_general | solution.py:29
  100.8 0.0 all-gather.5.cloned.1.call-start
  100.9 0.6 copy-done
  101.5 0.1 copy.23
  101.5 0.1 eq.10
  101.7 0.1 copy.24
  101.8 0.1 mul.14
  101.9 41.5 %reduce-scatter.3.cloned.1.call-done = f32[128,2048]{1,0:T(8,128)} async-done(((f32[512,2048]{1,0:T(8,128)}), f32[128,2048]{1,0:T(8,128)}) %reduce-scatter.3.cloned.1.call-update) | async-done | bytes 1048592 | tf_op jit(solution)/shard_map/reduce_scatter | solution.py:28
  143.5 1.4 reduce_max.9
  144.8 21.4 %pmax.7 = f32[128]{0:T(128)S(1)} all-reduce(f32[128]{0:T(128)S(1)} %reduce_max.9), channel_id=1, replica_groups=mesh['ctx'=4,'vocab'=8] {'vocab'}, use_global_device_ids=true, to_apply=%region_2.3 | all-reduce | flops 128 | bytes 1024 | tf_op jit(solution)/shard_map/pmax | solution.py:38
  166.2 1.6 fusion.4
  167.8 17.1 %all-reduce = (f32[128]{0:T(128)S(1)}, f32[128]{0:T(128)S(1)}) all-reduce(f32[128]{0:T(128)S(1)} %get-tuple-element.11, f32[128]{0:T(128)S(1)} %get-tuple-element.10), channel_id=1, replica_groups=mesh['ctx'=4,'vocab'=8] {'vocab'}, use_global_device_ids=true, to_apply=%region_6.7 | all-reduce | flops 256 | bytes 2048 | tf_op jit(solution)/shard_map/psum | solution.py:40
  184.9 2.4 fusion.3
  187.4 0.0 reduce-scatter.5.cloned.1.call-start
  187.4 20.4 %all-gather.5.cloned.1.call-done = bf16[512,2048]{1,0:T(8,128)(2,1)} async-done(((bf16[128,2048]{1,0:T(8,128)(2,1)}), bf16[512,2048]{1,0:T(8,128)(2,1)}) %all-gather.5.cloned.1.call-update) | async-done | bytes 2097168 | tf_op jit(solution)/shard_map/all_gather | solution.py:48
  207.9 7.7 %fusion.6 = f32[512,1792]{1,0:T(8,128)S(1)} fusion(bf16[512,2048]{1,0:T(8,128)(2,1)} %all-gather.5.cloned.1.call-done, bf16[1792,2048]{1,0:T(8,128)(2,1)} %param.5), kind=kOutput, calls=%fused_computation.16 | convolution fusion | flops 3758096384 | bytes 13107200 | tf_op jit(solution)/shard_map/dot_general | solution.py:47
  215.6 0.3 slice_bitcast_fusion.3
  215.9 0.4 pad_maximum_fusion
  216.2 45.9 %all_to_all.25 = f32[4,128,1792]{2,1,0:T(8,128)} all-to-all(f32[4,128,1792]{2,1,0:T(8,128)S(1)} %pad_maximum_fusion), channel_id=1, replica_groups=mesh['ctx'=4,'vocab'=8] {'ctx'}, dimensions={0} | all-to-all | bytes 7340032 | tf_op jit(solution)/shard_map/all_to_all | solution.py:7
  262.1 5.1 %copy.25 = f32[128,4,1792]{0,2,1:T(8,128)} copy(f32[128,4,1792]{2,0,1:T(8,128)} %bitcast.18) | data formatting | bytes 7340032 | tf_op jit(solution)/shard_map/reshape | solution.py:6
  267.3 0.1 reshape.27
  267.4 0.6 copy.27
  268.1 80.7 %reduce-scatter.5.cloned.1.call-done = f32[128,896]{0,1:T(8,128)} async-done(((f32[128,7168]{0,1:T(8,128)}), f32[128,896]{0,1:T(8,128)}) %reduce-scatter.5.cloned.1.call-update) | async-done | bytes 458768 | tf_op jit(solution)/shard_map/reduce_scatter | solution.py:54
  348.8 1.0 convert_element_type.11
  349.8 0.2 copy.26
  350.0 0.8 reshape.30
  (10 shorter events, 0.1 us)
Async XLA Ops:
  7.2 52.9 %all-gather.3.cloned.1.call-start = ((), (), s32[]{:S(2)}) async-start(), calls=%async_computation.4 | async-start | bytes 2064384 | tf_op jit(solution)/shard_map/all_gather | solution.py:26
  8.9 134.5 %reduce-scatter.3.cloned.1.call-start = ((), (), s32[]{:S(2)}) async-start(), calls=%async_computation.5 | async-start | bytes 5242880 | tf_op jit(solution)/shard_map/reduce_scatter | solution.py:28
  100.8 0.7 copy-start
  100.8 0.9 copy-start.1
  100.8 107.1 %all-gather.5.cloned.1.call-start = ((), (), s32[]{:S(2)}) async-start(), calls=%async_computation.6 | async-start | bytes 2621440 | tf_op jit(solution)/shard_map/all_gather | solution.py:48
  187.4 161.4 %reduce-scatter.5.cloned.1.call-start = ((), (), s32[]{:S(2)}) async-start(), calls=%async_computation.7 | async-start | bytes 4128768 | tf_op jit(solution)/shard_map/reduce_scatter | solution.py:54
Sparse Core Ops, SparseCore 0:
  10.8 49.2 all-gather.2
  100.9 42.4 reduce-scatter.2
  187.5 20.3 all-gather.4
  267.4 81.2 reduce-scatter.4
